TPU v7x, 32 devices: a whole 2x2x4 slice. The times are simulated.
32 devices in a mesh: fsdp: 16 (over z, y, x), rep: 2 (over core).
Axes of the slice: x: 2, y: 2, z: 4, core: 2. Of those that a mesh axis runs over, the one named last changes fastest.
Arguments:
- params: float32 [1536, 3584], P(('fsdp', 'rep')), may hold values from -6 to 6
- grads: bfloat16 [1536, 3584], P(('fsdp', 'rep')), may hold values from -6 to 6
- moments: bfloat16 [3, 1536, 3584], P(None, ('fsdp', 'rep')), may hold values from -6 to 6
- row_acc: float32 [1536], P(('fsdp', 'rep')), may hold values from 0.05 to 1
- lengths: int32 [32], replicated, may hold values from 1 to 384, 1536 in all
- tensor_order: int32 [32], replicated, may hold values from 0 to 31, each once
- col_acc: float32 [32, 3584], P('fsdp'), may hold values from 0.05 to 1
- hidden_state: float32 [32, 512], P('fsdp'), may hold values from -1 to 1
- cell_state: float32 [32, 512], P('fsdp'), may hold values from -4 to 4
- lstm_in: bfloat16 [10, 2048], replicated, may hold values from -2 to 2
- lstm_rec: bfloat16 [512, 2048], replicated, may hold values from -0.25 to 0.25
- lstm_bias: float32 [2048], replicated, may hold values from -3 to 3
- hyper_first: bfloat16 [512, 256], replicated, may hold values from -0.25 to 0.25
- hyper_rest: bfloat16 [512, 128], replicated, may hold values from -0.25 to 0.25
Outputs:
- update: float32 [1536, 3584], P(('fsdp', 'rep'))
- row_new: float32 [1536], P(('fsdp', 'rep'))
- col_new: float32 [32, 3584], P('fsdp')
- hidden_new: float32 [32, 512], P('fsdp')
- cell_new: float32 [32, 512], P('fsdp')
Inputs may be any that keep to these rules, and one draw needn't show every extreme that they name: `lengths`: they sum to 1536; the largest is 384. `tensor_order`: owner slot i belongs to fsdp index i // 2; each tensor appears once.
All inputs are finite; a program needn't handle non-finite values.
Results may differ from a plain program's by a relative error of at most 0.019.
Values may be sent and summed in bfloat16 or wider, within the bound.
A program may use at most 64 MiB of HBM per device.

v0:
```python
import math
import jax
import jax.numpy as jnp
from jax import lax
from jax.sharding import PartitionSpec as P

EPSILON = 1e-06
DECAY_RATE = 0.9


def owner_step(
    col_sums,
    tensor_stats,
    row_lengths,
    col_acc,
    hidden_state,
    cell_state,
    lstm_in,
    lstm_rec,
    lstm_bias,
    hyper_first,
    hyper_rest,
):
    col_width = col_acc.shape[1]
    col_new = DECAY_RATE * col_acc + (1.0 - DECAY_RATE) * col_sums / row_lengths[:, None]
    tensor_means = tensor_stats / (row_lengths * col_width)[:, None]
    log_means = jnp.log(tensor_means[:, :5] + EPSILON)
    corr_first = tensor_means[:, 5] / jnp.sqrt(tensor_means[:, 0] * tensor_means[:, 1] + EPSILON)
    corr_second = tensor_means[:, 6] / jnp.sqrt(tensor_means[:, 0] * tensor_means[:, 3] + EPSILON)
    corr_third = tensor_means[:, 7] / jnp.sqrt(tensor_means[:, 1] * tensor_means[:, 3] + EPSILON)
    col_mean = jnp.mean(col_new, axis=1)
    col_square = jnp.mean(col_new * col_new, axis=1)
    spread = jnp.log(col_square / (col_mean * col_mean))
    extra = jnp.stack(
        [corr_first, corr_second, corr_third, jnp.log(col_mean + EPSILON), spread], axis=1
    )
    features = jnp.concatenate([log_means, extra], axis=1).astype(jnp.bfloat16)
    gate_sum = jnp.dot(features, lstm_in, preferred_element_type=jnp.float32)
    gate_sum = (
        gate_sum
        + jnp.dot(hidden_state.astype(jnp.bfloat16), lstm_rec, preferred_element_type=jnp.float32)
        + lstm_bias
    )
    hid_width = hidden_state.shape[1]
    gate_in = gate_sum[:, :hid_width]
    gate_forget = gate_sum[:, hid_width : 2 * hid_width]
    gate_cand = gate_sum[:, 2 * hid_width : 3 * hid_width]
    gate_out = gate_sum[:, 3 * hid_width :]
    cell_new = jax.nn.sigmoid(gate_forget) * cell_state + jax.nn.sigmoid(gate_in) * jnp.tanh(
        gate_cand
    )
    hidden_new = jax.nn.sigmoid(gate_out) * jnp.tanh(cell_new)
    hidden_bf = hidden_new.astype(jnp.bfloat16)
    gen_first = jnp.dot(hidden_bf, hyper_first, preferred_element_type=jnp.float32).astype(
        jnp.bfloat16
    )
    gen_rest = jnp.dot(hidden_bf, hyper_rest, preferred_element_type=jnp.float32).astype(
        jnp.bfloat16
    )
    tensor_scales = jnp.stack(
        [
            jnp.sqrt(tensor_means[:, 0] + EPSILON),
            jnp.sqrt(tensor_means[:, 1] + EPSILON),
            jnp.sqrt(tensor_means[:, 4] + EPSILON),
            col_mean,
        ],
        axis=1,
    )
    return (col_new, hidden_new, cell_new, gen_first, gen_rest, tensor_scales)


def param_block(
    param_rows, grad_rows, moment_rows, row_var, col_rows, first_rows, rest_rows, scale_rows
):
    block_rows = param_rows.shape[0]
    grad_f = grad_rows.astype(jnp.float32)
    mom_f = moment_rows.astype(jnp.float32)
    v_factored = row_var[:, None] * col_rows / scale_rows[:, 3:4]
    inv_rms = lax.rsqrt(v_factored + EPSILON)
    grad_norm = grad_f * inv_rms
    mom_norm = mom_f[0] * inv_rms
    inputs = jnp.stack(
        [
            grad_norm,
            mom_norm,
            mom_f[1] * inv_rms,
            mom_f[2] * inv_rms,
            grad_f / scale_rows[:, 0:1],
            mom_f[0] / scale_rows[:, 1:2],
            param_rows / scale_rows[:, 2:3],
            grad_norm * mom_norm,
        ],
        axis=1,
    ).astype(jnp.bfloat16)
    hm_width = rest_rows.shape[1] // 4
    w_first = first_rows.reshape(block_rows, 8, hm_width)
    bias_first = rest_rows[:, :hm_width].astype(jnp.float32)
    w_second = rest_rows[:, hm_width:].reshape(block_rows, hm_width, 3)
    hidden_units = (
        jnp.einsum("bfc,bfh->bhc", inputs, w_first, preferred_element_type=jnp.float32)
        + bias_first[:, :, None]
    )
    hidden_units = jax.nn.relu(hidden_units).astype(jnp.bfloat16)
    mlp_out = jnp.einsum("bhc,bho->boc", hidden_units, w_second, preferred_element_type=jnp.float32)
    return mlp_out[:, 0] * jnp.exp(jnp.tanh(mlp_out[:, 1])) * jax.nn.sigmoid(mlp_out[:, 2])


def on_device(
    params,
    grads,
    moments,
    row_acc,
    lengths,
    tensor_order,
    col_acc,
    hidden_state,
    cell_state,
    lstm_in,
    lstm_rec,
    lstm_bias,
    hyper_first,
    hyper_rest,
):
    row_count = params.shape[0]
    tensor_count = lengths.shape[0]
    own_count = col_acc.shape[0]
    first_row = (lax.axis_index("fsdp") * lax.axis_size("rep") + lax.axis_index("rep")) * row_count
    tensor_ends = jnp.cumsum(lengths)
    global_rows = first_row + lax.iota(jnp.int32, row_count)
    seg_ids = jnp.sum((global_rows[:, None] >= tensor_ends[None, :]).astype(jnp.int32), axis=1)
    row_pick = (seg_ids[:, None] == tensor_order[None, :]).astype(jnp.float32)
    slot_match = tensor_order[:, None] == lax.iota(jnp.int32, tensor_count)[None, :]
    row_lengths = jnp.sum(jnp.where(slot_match, lengths[None, :], 0), axis=1).astype(jnp.float32)
    grad_f = grads.astype(jnp.float32)
    grad_sq = grad_f * grad_f
    row_new = DECAY_RATE * row_acc + (1.0 - DECAY_RATE) * jnp.mean(grad_sq, axis=1)
    mom_zero = moments[0].astype(jnp.float32)
    mom_one = moments[1].astype(jnp.float32)
    mom_two = moments[2].astype(jnp.float32)
    per_row = jnp.stack(
        [
            jnp.sum(grad_sq, axis=1),
            jnp.sum(mom_zero * mom_zero, axis=1),
            jnp.sum(mom_one * mom_one, axis=1),
            jnp.sum(mom_two * mom_two, axis=1),
            jnp.sum(params * params, axis=1),
            jnp.sum(grad_f * mom_zero, axis=1),
            jnp.sum(grad_f * mom_two, axis=1),
            jnp.sum(mom_zero * mom_two, axis=1),
        ],
        axis=1,
    )
    slot_stats = jnp.einsum("ri,rk->ik", row_pick, per_row, precision=lax.Precision.HIGHEST)
    slot_cols = jnp.einsum("ri,rc->ic", row_pick, grad_sq, precision=lax.Precision.HIGHEST)
    mine_start = lax.axis_index("fsdp") * own_count
    col_total, stats_total = lax.psum((slot_cols, slot_stats), ("fsdp", "rep"))
    col_prev, hidden_all, cell_all = (
        lax.all_gather(col_acc, "fsdp", axis=0, tiled=True),
        lax.all_gather(hidden_state, "fsdp", axis=0, tiled=True),
        lax.all_gather(cell_state, "fsdp", axis=0, tiled=True),
    )
    col_all, hidden_every, cell_every, first_all, rest_all, scale_all = owner_step(
        col_total,
        stats_total,
        row_lengths,
        col_prev,
        hidden_all,
        cell_all,
        lstm_in,
        lstm_rec,
        lstm_bias,
        hyper_first,
        hyper_rest,
    )
    col_new = lax.dynamic_slice_in_dim(col_all, mine_start, own_count, 0)
    hidden_new = lax.dynamic_slice_in_dim(hidden_every, mine_start, own_count, 0)
    cell_new = lax.dynamic_slice_in_dim(cell_every, mine_start, own_count, 0)
    col_rows = jnp.dot(row_pick, col_all, precision=lax.Precision.HIGHEST)
    scale_rows = jnp.dot(row_pick, scale_all, precision=lax.Precision.HIGHEST)
    pick_bf = row_pick.astype(jnp.bfloat16)
    first_rows = jnp.dot(pick_bf, first_all, preferred_element_type=jnp.float32).astype(
        jnp.bfloat16
    )
    rest_rows = jnp.dot(pick_bf, rest_all, preferred_element_type=jnp.float32).astype(jnp.bfloat16)
    block_rows = math.gcd(row_count, 16)
    block_count = row_count // block_rows

    def one_block(index):
        start = index * block_rows
        return param_block(
            lax.dynamic_slice_in_dim(params, start, block_rows, 0),
            lax.dynamic_slice_in_dim(grads, start, block_rows, 0),
            lax.dynamic_slice_in_dim(moments, start, block_rows, 1),
            lax.dynamic_slice_in_dim(row_new, start, block_rows, 0),
            lax.dynamic_slice_in_dim(col_rows, start, block_rows, 0),
            lax.dynamic_slice_in_dim(first_rows, start, block_rows, 0),
            lax.dynamic_slice_in_dim(rest_rows, start, block_rows, 0),
            lax.dynamic_slice_in_dim(scale_rows, start, block_rows, 0),
        )

    update = lax.map(one_block, lax.iota(jnp.int32, block_count)).reshape(params.shape)
    return (update, row_new, col_new, hidden_new, cell_new)


def solution(mesh):
    placed = (
        P(("fsdp", "rep"), None),
        P(("fsdp", "rep"), None),
        P(None, ("fsdp", "rep"), None),
        P(("fsdp", "rep")),
        P(),
        P(),
        P("fsdp", None),
        P("fsdp", None),
        P("fsdp", None),
        P(),
        P(),
        P(),
        P(),
        P(),
    )
    return jax.shard_map(
        on_device,
        mesh=mesh,
        in_specs=placed,
        out_specs=(
            P(("fsdp", "rep"), None),
            P(("fsdp", "rep")),
            P("fsdp", None),
            P("fsdp", None),
            P("fsdp", None),
        ),
        check_vma=False,
    )
```

profile of v0, /device:TPU:0, one launch (start us, length us, event | category | flops | bytes accessed | tf_op | source)
XLA Modules:
  0.0 245.1 jit_solution(586881530292995540)
XLA Ops:
  7.3 0.9 copy.76
  8.4 2.3 fusion.25
  10.7 0.9 select_reduce_fusion
  11.6 1.2 multiply_reduce_fusion.1
  12.7 1.7 fusion.30
  14.4 1.2 multiply_reduce_fusion
  16.5 42.0 %psum.14 = f32[32,8]{0,1:T(8,128)S(1)} all-reduce(f32[32,8]{0,1:T(8,128)S(1)} %fusion.50), channel_id=1, replica_groups=mesh['fsdp'=16,'rep'=2] {'fsdp','rep'}, use_global_device_ids=true, to_apply=%region_12.13 | all-reduce | flops 256 | bytes 2048 | tf_op jit(solution)/shard_map/psum | solution.py:156
  59.1 39.8 %all-gather.1 = bf16[16,2,512]{2,1,0:T(2,128)(2,1)S(1)} all-gather(bf16[1,2,512]{2,1,0:T(2,128)(2,1)S(1)} %bitcast_convert_fusion), channel_id=1, replica_groups=mesh['fsdp'=16,'rep'=2] {'fsdp'}, dimensions={0}, use_global_device_ids=true | all-gather | bytes 34816 | tf_op jit(solution)/shard_map/all_gather | solution.py:159
  98.9 38.4 %all-gather = f32[16,2,3584]{2,1,0:T(2,128)S(1)} all-gather(f32[1,2,3584]{2,1,0:T(2,128)S(1)} %bitcast.121), channel_id=1, replica_groups=mesh['fsdp'=16,'rep'=2] {'fsdp'}, dimensions={0}, use_global_device_ids=true | all-gather | bytes 487424 | tf_op jit(solution)/shard_map/all_gather | solution.py:158
  138.1 37.8 %all-gather.2 = f32[16,2,512]{2,1,0:T(2,128)S(1)} all-gather(f32[1,2,512]{2,1,0:T(2,128)S(1)} %bitcast.122), channel_id=1, replica_groups=mesh['fsdp'=16,'rep'=2] {'fsdp'}, dimensions={0}, use_global_device_ids=true | all-gather | bytes 69632 | tf_op jit(solution)/shard_map/all_gather | solution.py:160
  176.9 1.3 multiply_reduce_fusion.2
  178.2 2.0 fusion.47
  182.7 0.9 convolution_convert_fusion
  183.8 54.4 %while.10 = (s32[]{:T(128)}, f32[3,16,3584]{2,1,0:T(8,128)}, s32[3]{0:T(128)S(1)}, bf16[48,128]{1,0:T(8,128)(2,1)S(1)}, bf16[48,256]{1,0:T(8,128)(2,1)}, /*index...) while((s32[]{:T(128)}, f32[3,16,3584]{2,1,0:T(8,128)}, ...), condition=%wide.region_16.17_spmd, body=%wide.region_15.16_spmd.sunk | while | flops 47481352 | bytes 11314883 | solution.py:201
  187.0 1.0 dynamic-slice_convert_fusion.4
  188.4 1.3 fusion.104
  190.6 0.9 copy.132
  191.5 0.9 copy.133
  192.4 5.5 %stack.83 = bf16[16,8,3584]{2,1,0:T(8,128)(2,1)} concatenate(bf16[16,1,3584]{2,1,0:T(2,128)(2,1)S(1)} %copy.127, bf16[16,1,3584]{2,1,0:T(2,128)(2,1)S(1)} %copy.128, bf16[16,1,3584]{2,1,0:T(2,128)(2,1)S(1)} %copy.129, bf16[16,1,3584]{2,1,0:T(2,128)(2,1)S(1)} %copy.130, bf16[16,1,3584]{2,1,0:T(2,128)(2,1)S(1)} %copy.131, bf16[16,1,3584]{2,1,0:T(2,128)(2,1)S(1)} %fusion.105, ...), dimensions={1} | concatenate | bytes 1835008 | tf_op jit(solution)/shard_map/while/body/eval_jaxpr/stack | solution.py:82
  197.9 2.8 %fusion.106 = f32[16,3,3584]{2,1,0:T(4,128)S(1)} fusion(bf16[16,32,3]{1,2,0:T(4,128)(2,1)S(1)} %copy.126, bf16[16,8,32]{2,1,0:T(8,128)(2,1)S(1)} %reshape.216, bf16[16,8,3584]{2,1,0:T(8,128)(2,1)} %stack.83, f32[16,32]{1,0:T(8,128)S(1)} %dynamic-slice_convert_fusion.5), kind=kOutput, calls=%fused_computation.1.clone.1 | convolution fusion | flops 45875200 | bytes 1618944 | tf_op jit(solution)/shard_map/while/body/eval_jaxpr/bhc,bho->boc/dot_general | solution.py:104
  205.2 1.0 dynamic-slice_convert_fusion.4
  206.5 1.3 fusion.104
  208.8 0.9 copy.132
  209.7 0.9 copy.133
  210.5 5.5 %stack.83 = bf16[16,8,3584]{2,1,0:T(8,128)(2,1)} concatenate(bf16[16,1,3584]{2,1,0:T(2,128)(2,1)S(1)} %copy.127, bf16[16,1,3584]{2,1,0:T(2,128)(2,1)S(1)} %copy.128, bf16[16,1,3584]{2,1,0:T(2,128)(2,1)S(1)} %copy.129, bf16[16,1,3584]{2,1,0:T(2,128)(2,1)S(1)} %copy.130, bf16[16,1,3584]{2,1,0:T(2,128)(2,1)S(1)} %copy.131, bf16[16,1,3584]{2,1,0:T(2,128)(2,1)S(1)} %fusion.105, ...), dimensions={1} | concatenate | bytes 1835008 | tf_op jit(solution)/shard_map/while/body/eval_jaxpr/stack | solution.py:82
  216.0 2.8 %fusion.106 = f32[16,3,3584]{2,1,0:T(4,128)S(1)} fusion(bf16[16,32,3]{1,2,0:T(4,128)(2,1)S(1)} %copy.126, bf16[16,8,32]{2,1,0:T(8,128)(2,1)S(1)} %reshape.216, bf16[16,8,3584]{2,1,0:T(8,128)(2,1)} %stack.83, f32[16,32]{1,0:T(8,128)S(1)} %dynamic-slice_convert_fusion.5), kind=kOutput, calls=%fused_computation.1.clone.1 | convolution fusion | flops 45875200 | bytes 1618944 | tf_op jit(solution)/shard_map/while/body/eval_jaxpr/bhc,bho->boc/dot_general | solution.py:104
  223.3 1.0 dynamic-slice_convert_fusion.4
  224.7 1.3 fusion.104
  226.9 0.9 copy.132
  227.8 0.9 copy.133
  228.7 5.5 %stack.83 = bf16[16,8,3584]{2,1,0:T(8,128)(2,1)} concatenate(bf16[16,1,3584]{2,1,0:T(2,128)(2,1)S(1)} %copy.127, bf16[16,1,3584]{2,1,0:T(2,128)(2,1)S(1)} %copy.128, bf16[16,1,3584]{2,1,0:T(2,128)(2,1)S(1)} %copy.129, bf16[16,1,3584]{2,1,0:T(2,128)(2,1)S(1)} %copy.130, bf16[16,1,3584]{2,1,0:T(2,128)(2,1)S(1)} %copy.131, bf16[16,1,3584]{2,1,0:T(2,128)(2,1)S(1)} %fusion.105, ...), dimensions={1} | concatenate | bytes 1835008 | tf_op jit(solution)/shard_map/while/body/eval_jaxpr/stack | solution.py:82
  234.2 2.8 %fusion.106 = f32[16,3,3584]{2,1,0:T(4,128)S(1)} fusion(bf16[16,32,3]{1,2,0:T(4,128)(2,1)S(1)} %copy.126, bf16[16,8,32]{2,1,0:T(8,128)(2,1)S(1)} %reshape.216, bf16[16,8,3584]{2,1,0:T(8,128)(2,1)} %stack.83, f32[16,32]{1,0:T(8,128)S(1)} %dynamic-slice_convert_fusion.5), kind=kOutput, calls=%fused_computation.1.clone.1 | convolution fusion | flops 45875200 | bytes 1618944 | tf_op jit(solution)/shard_map/while/body/eval_jaxpr/bhc,bho->boc/dot_general | solution.py:104
  (116 shorter events, 21.2 us)
Async XLA Ops:
  7.2 130.4 %copy-start = (bf16[512,2048]{1,0:T(8,128)(2,1)S(1)}, bf16[512,2048]{1,0:T(8,128)(2,1)}, u32[]{:S(2)}) copy-start(bf16[512,2048]{1,0:T(8,128)(2,1)} %param.26) | copy-start | bytes 6291460
  7.2 9.1 %copy-start.6 = (s32[32]{0:T(128)S(1)}, s32[32]{0:T(128)}, u32[]{:S(2)}) copy-start(s32[32]{0:T(128)} %param.21) | copy-start | bytes 388
  7.2 8.5 %copy-start.10 = (f32[2,512]{1,0:T(2,128)S(1)}, f32[2,512]{1,0:T(2,128)}, u32[]{:S(2)}) copy-start(f32[2,512]{1,0:T(2,128)} %param.23) | copy-start | bytes 12292
  7.2 8.5 %copy-start.11 = (f32[48]{0:T(128)S(1)}, f32[48]{0:T(128)}, u32[]{:S(2)}) copy-start(f32[48]{0:T(128)} %param.19) | copy-start | bytes 580
  7.2 91.7 %copy-start.4 = (f32[2,3584]{1,0:T(2,128)S(1)}, f32[2,3584]{1,0:T(2,128)}, u32[]{:S(2)}) copy-start(f32[2,3584]{1,0:T(2,128)} %param.22) | copy-start | bytes 86020
  7.2 169.6 %all-reduce.2.cloned.1.call-start = ((), (), s32[]{:S(2)}) async-start(), calls=%async_computation | async-start | bytes 917504 | tf_op jit(solution)/shard_map/psum | solution.py:156
  8.4 7.9 %copy-start.7 = (s32[48]{0:T(128)}, s32[48]{0:T(128)S(1)}, u32[]{:S(2)}) copy-start(s32[48]{0:T(128)S(1)} %convert_reduce_fusion) | copy-start | bytes 580
  15.7 122.4 %copy-start.9 = (f32[2,512]{1,0:T(2,128)S(1)}, f32[2,512]{1,0:T(2,128)}, u32[]{:S(2)}) copy-start(f32[2,512]{1,0:T(2,128)} %param.24) | copy-start | bytes 12292
  138.0 43.5 %copy-start.3 = (bf16[10,2048]{1,0:T(8,128)(2,1)S(1)}, bf16[10,2048]{1,0:T(8,128)(2,1)}, u32[]{:S(2)}) copy-start(bf16[10,2048]{1,0:T(8,128)(2,1)} %param.25) | copy-start | bytes 122884
  138.0 43.5 %copy-start.5 = (f32[2048]{0:T(1024)S(1)}, f32[2048]{0:T(1024)}, u32[]{:S(2)}) copy-start(f32[2048]{0:T(1024)} %param.27) | copy-start | bytes 24580
  176.5 6.0 %copy-start.2 = (bf16[512,128]{1,0:T(8,128)(2,1)S(1)}, bf16[512,128]{1,0:T(8,128)(2,1)}, u32[]{:S(2)}) copy-start(bf16[512,128]{1,0:T(8,128)(2,1)} %param.29) | copy-start | bytes 393220
  176.8 5.7 %copy-start.8 = (s32[48]{0:T(128)S(1)}, s32[48]{0:T(128)}, u32[]{:S(2)}) copy-start(s32[48]{0:T(128)} %copy-done.7) | copy-start | bytes 580
  176.8 5.9 %copy-start.1 = (bf16[512,256]{1,0:T(8,128)(2,1)S(1)}, bf16[512,256]{1,0:T(8,128)(2,1)}, u32[]{:S(2)}) copy-start(bf16[512,256]{1,0:T(8,128)(2,1)} %param.28) | copy-start | bytes 786436
Sparse Core Ops, SparseCore 0:
  13.3 130.1 all-reduce.1
where the time goes:
time: 247 us; the launch traced here: 245 us
  blocking collectives  158 us (64%)
  local copies, waits for them, and re-layouts  36.7 us (15%)
  other arithmetic  19 us (8%)
  matrix products  14.8 us (6%)
  between operations  14.3 us (6%)
    psum x1, blocking collectives, on_device(): col_total, stats_total = lax.psum((slot_cols, slot_stats), ('fsdp', 'rep'))  42 us
    all_gather x1, blocking collectives, on_device(): lax.all_gather(hidden_state, 'fsdp', axis=0, tiled=True)  39.8 us
    all_gather x1, blocking collectives, on_device(): lax.all_gather(col_acc, 'fsdp', axis=0, tiled=True)  38.4 us
    all_gather x1, blocking collectives, on_device(): lax.all_gather(cell_state, 'fsdp', axis=0, tiled=True)  37.8 us
    another operation x24, local copies, waits for them, and re-layouts, param_block(): jnp.stack([grad_norm, mom_norm, mom_f[1] * inv_rms, mom_f[2] * inv_rms, g...  24.4 us
    dot_general x3, matrix products, param_block(): jnp.einsum('bhc,bho->boc', hidden_units, w_second, preferred_element_type...  8.4 us
  transfers between devices with their start and end apart: 1, of which 0 were waited for; matrix products, arithmetic and copies ran while one was open for 3% of the time, Pallas kernels for 0%

commit v1 on v0

--- a/solution.py
+++ b/solution.py
@@ -153,7 +153,7 @@
     slot_stats = jnp.einsum("ri,rk->ik", row_pick, per_row, precision=lax.Precision.HIGHEST)
     slot_cols = jnp.einsum("ri,rc->ic", row_pick, grad_sq, precision=lax.Precision.HIGHEST)
     mine_start = lax.axis_index("fsdp") * own_count
-    col_total, stats_total = lax.psum((slot_cols, slot_stats), ("fsdp", "rep"))
+    col_total, stats_total = lax.psum(lax.psum((slot_cols, slot_stats), "rep"), "fsdp")
     col_prev, hidden_all, cell_all = (
         lax.all_gather(col_acc, "fsdp", axis=0, tiled=True),
         lax.all_gather(hidden_state, "fsdp", axis=0, tiled=True),

time: 247 us -> 346 us (1.40)
  waiting for transfers between devices: 0.04 us -> 106 us
  local copies, waits for them, and re-layouts: 36.7 us -> 32.5 us
    psum x1 -> x2, waiting for transfers between devices: 0.02 us -> 106 us  [the longest x1 106 us: on_device(): lax.psum(lax.psum((slot_cols, slot_stats), 'rep'), 'fsdp')]
    all_gather x1, blocking collectives: 39.8 us -> 35.6 us  [on_device(): lax.all_gather(hidden_state, 'fsdp', axis=0, tiled=True)]
    psum x1 -> x2, blocking collectives: 42 us -> 46 us  [the longest x1 43.3 us: on_device(): lax.psum(lax.psum((slot_cols, slot_stats), 'rep'), 'fsdp')]
  transfers between devices with their start and end apart: 1 -> 2, of which waited for: 0 -> 1; matrix products, arithmetic and copies ran while one was open for 3% -> 2% of each run, Pallas kernels for 0% -> 0%
where the time goes in v1:
time: 346 us; the launch traced here: 344 us
  blocking collectives  158 us (46%)
  waiting for transfers between devices  106 us (31%)
  local copies, waits for them, and re-layouts  32.5 us (9%)
  other arithmetic  17.3 us (5%)
  between operations  14.3 us (4%)
  matrix products  13.6 us (4%)
    psum x1, waiting for transfers between devices, on_device(): lax.psum(lax.psum((slot_cols, slot_stats), 'rep'), 'fsdp')  106 us
    psum x1, blocking collectives, on_device(): lax.psum(lax.psum((slot_cols, slot_stats), 'rep'), 'fsdp')  43.3 us
    all_gather x1, blocking collectives, on_device(): lax.all_gather(col_acc, 'fsdp', axis=0, tiled=True)  40.2 us
    all_gather x1, blocking collectives, on_device(): lax.all_gather(cell_state, 'fsdp', axis=0, tiled=True)  35.8 us
    all_gather x1, blocking collectives, on_device(): lax.all_gather(hidden_state, 'fsdp', axis=0, tiled=True)  35.6 us
    another operation x24, local copies, waits for them, and re-layouts, param_block(): jnp.stack([grad_norm, mom_norm, mom_f[1] * inv_rms, mom_f[2] * inv_rms, g...  24.4 us
    dot_general x3, matrix products, param_block(): jnp.einsum('bhc,bho->boc', hidden_units, w_second, preferred_element_type...  8.42 us
  transfers between devices with their start and end apart: 2, of which 1 were waited for; matrix products, arithmetic and copies ran while one was open for 2% of the time, Pallas kernels for 0%

profile of v1, /device:TPU:0, one launch (start us, length us, event | category | flops | bytes accessed | tf_op | source)
XLA Modules:
  0.0 344.0 jit_solution(4265317031800695102)
XLA Ops:
  7.3 0.9 copy.76
  8.4 2.3 fusion.25
  11.6 1.2 multiply_reduce_fusion.1
  12.8 1.7 fusion.30
  14.5 1.2 multiply_reduce_fusion
  16.0 2.6 psum.28
  18.6 43.3 %psum.29 = f32[32,8]{0,1:T(8,128)S(1)} all-reduce(f32[32,8]{0,1:T(8,128)S(1)} %psum.28), channel_id=1, replica_groups=mesh['fsdp'=16,'rep'=2] {'fsdp'}, use_global_device_ids=true, to_apply=%region_14.15 | all-reduce | flops 256 | bytes 2048 | tf_op jit(solution)/shard_map/psum | solution.py:156
  62.0 35.8 %all-gather.2 = f32[16,2,512]{2,1,0:T(2,128)S(1)} all-gather(f32[1,2,512]{2,1,0:T(2,128)S(1)} %bitcast.122), channel_id=1, replica_groups=mesh['fsdp'=16,'rep'=2] {'fsdp'}, dimensions={0}, use_global_device_ids=true | all-gather | bytes 69632 | tf_op jit(solution)/shard_map/all_gather | solution.py:160
  97.8 40.2 %all-gather = f32[16,2,3584]{2,1,0:T(2,128)S(1)} all-gather(f32[1,2,3584]{2,1,0:T(2,128)S(1)} %bitcast.121), channel_id=1, replica_groups=mesh['fsdp'=16,'rep'=2] {'fsdp'}, dimensions={0}, use_global_device_ids=true | all-gather | bytes 487424 | tf_op jit(solution)/shard_map/all_gather | solution.py:158
  138.2 35.6 %all-gather.1 = bf16[16,2,512]{2,1,0:T(2,128)(2,1)S(1)} all-gather(bf16[1,2,512]{2,1,0:T(2,128)(2,1)S(1)} %bitcast_convert_fusion), channel_id=1, replica_groups=mesh['fsdp'=16,'rep'=2] {'fsdp'}, dimensions={0}, use_global_device_ids=true | all-gather | bytes 34816 | tf_op jit(solution)/shard_map/all_gather | solution.py:159
  174.9 106.3 %all-reduce.5.cloned.1.call-done = f32[32,3584]{1,0:T(8,128)} async-done(((f32[32,3584]{1,0:T(8,128)}), f32[32,3584]{1,0:T(8,128)}) %all-reduce.5.cloned.1.call-update) | async-done | bytes 458768 | tf_op jit(solution)/shard_map/psum | solution.py:156
  281.2 1.3 multiply_reduce_fusion.2
  282.5 1.4 fusion.47
  286.2 50.5 %while.10 = (s32[]{:T(128)}, f32[3,16,3584]{2,1,0:T(8,128)}, s32[3]{0:T(128)S(1)}, bf16[48,128]{1,0:T(8,128)(2,1)S(1)}, bf16[48,256]{1,0:T(8,128)(2,1)S(1)}, /*i...) while((s32[]{:T(128)}, f32[3,16,3584]{2,1,0:T(8,128)}, ...), condition=%wide.region_18.19_spmd, body=%wide.region_17.18_spmd.sunk | while | flops 47481352 | bytes 11511547 | solution.py:201
  288.1 1.0 dynamic-slice_convert_fusion.4
  289.5 1.3 fusion.104
  291.7 0.9 copy.132
  292.6 0.9 copy.133
  293.5 5.5 %stack.83 = bf16[16,8,3584]{2,1,0:T(8,128)(2,1)} concatenate(bf16[16,1,3584]{2,1,0:T(2,128)(2,1)S(1)} %copy.127, bf16[16,1,3584]{2,1,0:T(2,128)(2,1)S(1)} %copy.128, bf16[16,1,3584]{2,1,0:T(2,128)(2,1)S(1)} %copy.129, bf16[16,1,3584]{2,1,0:T(2,128)(2,1)S(1)} %copy.130, bf16[16,1,3584]{2,1,0:T(2,128)(2,1)S(1)} %copy.131, bf16[16,1,3584]{2,1,0:T(2,128)(2,1)S(1)} %fusion.105, ...), dimensions={1} | concatenate | bytes 1835008 | tf_op jit(solution)/shard_map/while/body/eval_jaxpr/stack | solution.py:82
  299.0 2.8 fusion.106
  304.9 1.0 dynamic-slice_convert_fusion.4
  306.3 1.3 fusion.104
  308.5 0.9 copy.132
  309.4 0.9 copy.133
  310.3 5.5 %stack.83 = bf16[16,8,3584]{2,1,0:T(8,128)(2,1)} concatenate(bf16[16,1,3584]{2,1,0:T(2,128)(2,1)S(1)} %copy.127, bf16[16,1,3584]{2,1,0:T(2,128)(2,1)S(1)} %copy.128, bf16[16,1,3584]{2,1,0:T(2,128)(2,1)S(1)} %copy.129, bf16[16,1,3584]{2,1,0:T(2,128)(2,1)S(1)} %copy.130, bf16[16,1,3584]{2,1,0:T(2,128)(2,1)S(1)} %copy.131, bf16[16,1,3584]{2,1,0:T(2,128)(2,1)S(1)} %fusion.105, ...), dimensions={1} | concatenate | bytes 1835008 | tf_op jit(solution)/shard_map/while/body/eval_jaxpr/stack | solution.py:82
  315.8 2.8 fusion.106
  321.7 1.0 dynamic-slice_convert_fusion.4
  323.1 1.3 fusion.104
  325.3 0.9 copy.132
  326.2 0.9 copy.133
  327.1 5.5 %stack.83 = bf16[16,8,3584]{2,1,0:T(8,128)(2,1)} concatenate(bf16[16,1,3584]{2,1,0:T(2,128)(2,1)S(1)} %copy.127, bf16[16,1,3584]{2,1,0:T(2,128)(2,1)S(1)} %copy.128, bf16[16,1,3584]{2,1,0:T(2,128)(2,1)S(1)} %copy.129, bf16[16,1,3584]{2,1,0:T(2,128)(2,1)S(1)} %copy.130, bf16[16,1,3584]{2,1,0:T(2,128)(2,1)S(1)} %copy.131, bf16[16,1,3584]{2,1,0:T(2,128)(2,1)S(1)} %fusion.105, ...), dimensions={1} | concatenate | bytes 1835008 | tf_op jit(solution)/shard_map/while/body/eval_jaxpr/stack | solution.py:82
  332.6 2.8 fusion.106
  (130 shorter events, 16.6 us)
Async XLA Ops:
  7.2 167.2 %copy-start = (bf16[512,2048]{1,0:T(8,128)(2,1)S(1)}, bf16[512,2048]{1,0:T(8,128)(2,1)}, u32[]{:S(2)}) copy-start(bf16[512,2048]{1,0:T(8,128)(2,1)} %param.26) | copy-start | bytes 6291460
  7.2 8.6 %copy-start.8 = (s32[32]{0:T(128)S(1)}, s32[32]{0:T(128)}, u32[]{:S(2)}) copy-start(s32[32]{0:T(128)} %param.21) | copy-start | bytes 388
  7.2 8.6 %copy-start.10 = (f32[2,512]{1,0:T(2,128)S(1)}, f32[2,512]{1,0:T(2,128)}, u32[]{:S(2)}) copy-start(f32[2,512]{1,0:T(2,128)} %param.23) | copy-start | bytes 12292
  7.2 54.8 %copy-start.9 = (f32[2,512]{1,0:T(2,128)S(1)}, f32[2,512]{1,0:T(2,128)}, u32[]{:S(2)}) copy-start(f32[2,512]{1,0:T(2,128)} %param.24) | copy-start | bytes 12292
  7.2 90.6 %copy-start.6 = (f32[2,3584]{1,0:T(2,128)S(1)}, f32[2,3584]{1,0:T(2,128)}, u32[]{:S(2)}) copy-start(f32[2,3584]{1,0:T(2,128)} %param.22) | copy-start | bytes 86020
  7.2 167.1 %all-reduce.3.cloned.1.call-start = ((), (), s32[]{:S(2)}) async-start(), calls=%async_computation | async-start | bytes 917504 | tf_op jit(solution)/shard_map/psum | solution.py:156
  10.7 270.5 %all-reduce.5.cloned.1.call-start = ((), (), s32[]{:S(2)}) async-start(), calls=%async_computation.1 | async-start | bytes 917504 | tf_op jit(solution)/shard_map/psum | solution.py:156
  14.5 159.9 %copy-start.11 = (f32[48]{0:T(128)S(1)}, f32[48]{0:T(128)}, u32[]{:S(2)}) copy-start(f32[48]{0:T(128)} %param.19) | copy-start | bytes 580
  174.4 110.2 %copy-start.5 = (bf16[10,2048]{1,0:T(8,128)(2,1)S(1)}, bf16[10,2048]{1,0:T(8,128)(2,1)}, u32[]{:S(2)}) copy-start(bf16[10,2048]{1,0:T(8,128)(2,1)} %param.25) | copy-start | bytes 122884
  174.4 110.2 %copy-start.7 = (f32[2048]{0:T(1024)S(1)}, f32[2048]{0:T(1024)}, u32[]{:S(2)}) copy-start(f32[2048]{0:T(1024)} %param.27) | copy-start | bytes 24580
  174.9 110.6 %copy-start.4 = (bf16[512,128]{1,0:T(8,128)(2,1)S(1)}, bf16[512,128]{1,0:T(8,128)(2,1)}, u32[]{:S(2)}) copy-start(bf16[512,128]{1,0:T(8,128)(2,1)} %param.29) | copy-start | bytes 393220
  174.9 110.9 %copy-start.1 = (bf16[512,256]{1,0:T(8,128)(2,1)S(1)}, bf16[512,256]{1,0:T(8,128)(2,1)}, u32[]{:S(2)}) copy-start(bf16[512,256]{1,0:T(8,128)(2,1)} %param.28) | copy-start | bytes 786436
  286.2 4.6 %copy-start.2 = (bf16[48,256]{1,0:T(8,128)(2,1)}, bf16[48,256]{1,0:T(8,128)(2,1)S(1)}, u32[]{:S(2)}) copy-start(bf16[48,256]{1,0:T(8,128)(2,1)S(1)} %get-tuple-element.295) | copy-start | bytes 73732 | tf_op jit(solution)/shard_map/while
  299.0 4.1 %copy-start.3 = (bf16[48,256]{1,0:T(8,128)(2,1)S(1)}, bf16[48,256]{1,0:T(8,128)(2,1)}, u32[]{:S(2)}) copy-start(bf16[48,256]{1,0:T(8,128)(2,1)} %copy-done.2) | copy-start | bytes 73732 | tf_op jit(solution)/shard_map/while
  303.1 4.5 %copy-start.2 = (bf16[48,256]{1,0:T(8,128)(2,1)}, bf16[48,256]{1,0:T(8,128)(2,1)S(1)}, u32[]{:S(2)}) copy-start(bf16[48,256]{1,0:T(8,128)(2,1)S(1)} %get-tuple-element.295) | copy-start | bytes 73732 | tf_op jit(solution)/shard_map/while
  315.8 4.1 %copy-start.3 = (bf16[48,256]{1,0:T(8,128)(2,1)S(1)}, bf16[48,256]{1,0:T(8,128)(2,1)}, u32[]{:S(2)}) copy-start(bf16[48,256]{1,0:T(8,128)(2,1)} %copy-done.2) | copy-start | bytes 73732 | tf_op jit(solution)/shard_map/while
  319.9 4.5 %copy-start.2 = (bf16[48,256]{1,0:T(8,128)(2,1)}, bf16[48,256]{1,0:T(8,128)(2,1)S(1)}, u32[]{:S(2)}) copy-start(bf16[48,256]{1,0:T(8,128)(2,1)S(1)} %get-tuple-element.295) | copy-start | bytes 73732 | tf_op jit(solution)/shard_map/while
  332.6 4.1 %copy-start.3 = (bf16[48,256]{1,0:T(8,128)(2,1)S(1)}, bf16[48,256]{1,0:T(8,128)(2,1)}, u32[]{:S(2)}) copy-start(bf16[48,256]{1,0:T(8,128)(2,1)} %copy-done.2) | copy-start | bytes 73732 | tf_op jit(solution)/shard_map/while
  336.7 0.5 copy-start.12
Sparse Core Ops, SparseCore 0:
  10.8 21.2 all-reduce.2
  174.5 106.6 all-reduce.4
